TPU v7x, 32 devices: a whole 2x2x4 slice. The times are simulated.
32 devices in a mesh: groups: 1, ep: 16 (over z, y, x), hp: 2 (over core).
Axes of the slice: x: 2, y: 2, z: 4, core: 2. Of those that a mesh axis runs over, the one named last changes fastest.
Arguments:
- x_pre: bfloat16 [896, 1536], P(('groups', 'ep')), may hold values from -6 to 6
- x_dec: bfloat16 [128, 1536], P(('groups', 'ep')), may hold values from -6 to 6
- prefill_query_rows: bfloat16 [896, 2048], P(('groups', 'ep'), 'hp'), may hold values from -240 to 240
- prefill_key_values: bfloat16 [2, 896, 256], P(None, ('groups', 'ep'), 'hp'), may hold values from -6.1 to 6.1
- decode_query_rows: bfloat16 [128, 2048], P(('groups', 'ep'), 'hp'), may hold values from -240 to 240
- decode_key_values: bfloat16 [2, 128, 256], P(None, ('groups', 'ep'), 'hp'), may hold values from -6 to 6
- cache: bfloat16 [2, 128, 128, 256], P(None, ('groups', 'ep'), None, 'hp'), may hold values from -6.1 to 6.1
- cache_len: int32 [128], P(('groups', 'ep')), may hold values from 2 to 128
- sinks: float32 [32], P('hp'), may hold values from -1 to 5
- o_weight: bfloat16 [2048, 1536], P('hp', 'ep'), may hold values from -0.125 to 0.125
- norm_gain: float32 [1536], replicated, may hold values from 0.5 to 1.5
- expert_ids: int32 [1024, 4], P(('groups', 'ep')), may hold values from 0 to 7, all different within a row; in each aligned block of 64 rows (0 to 63, 64 to 127, ...) at most 48 rows name the same one
- route_logits: float32 [1024, 4], P(('groups', 'ep')), may hold values from -6 to 6
- w_gate_up: bfloat16 [16, 2, 1536, 768], P('ep', None, None, 'hp'), may hold values from -0.15625 to 0.15625
- w_down: bfloat16 [16, 768, 1536], P('ep', 'hp'), may hold values from -0.15625 to 0.15625
Outputs:
- layer_out: bfloat16 [1024, 1536], P(('groups', 'ep', 'hp'))
Inputs may be any that keep to these rules, and one draw needn't show every extreme that they name: `expert_ids`: each row names 4 different experts; among the rows of one index of ep no expert is named by more than 48 rows, and in every draw some expert is named by exactly 48 rows of some index.
All inputs are finite; a program needn't handle non-finite values.
Results may differ from a plain program's by a relative error of at most 0.0065.
Values may be sent and summed in bfloat16 or wider, within the bound.
A program may use at most 64 MiB of HBM per device.

v0:
```python
import functools

import jax
import jax.numpy as jnp
from jax import lax
from jax.experimental import pallas as pl
from jax.experimental.pallas import tpu as pltpu
from jax.sharding import PartitionSpec as P

HEAD_SIZE = 64


EPS = 1e-05


def softmax_probability(scores, sink_logit_bias):
    top = jnp.maximum(jnp.max(scores, axis=-1, keepdims=True), sink_logit_bias)
    expo = jnp.exp(scores - top)
    total = jnp.sum(expo, axis=-1, keepdims=True) + jnp.exp(sink_logit_bias - top)
    return (expo / total).astype(jnp.bfloat16)


def rms_norm(stream, gain):
    mean_sq = jnp.mean(stream * stream, axis=-1, keepdims=True)
    return (stream * lax.rsqrt(mean_sq + EPS) * gain).astype(jnp.bfloat16)


def attention_rows(
    x_pre,
    x_dec,
    prefill_query_rows,
    prefill_key_values,
    decode_query_rows,
    decode_key_values,
    cache,
    cache_len,
    sinks):
    pre_rows, width = x_pre.shape
    dec_rows = x_dec.shape[0]
    kv_heads = prefill_key_values.shape[2] // HEAD_SIZE
    q_heads = sinks.shape[0]
    head_group = q_heads // kv_heads
    kv_max = cache.shape[2]
    scale = HEAD_SIZE ** (-0.5)
    sink_logit_bias = sinks.reshape(kv_heads, head_group)[None, :, :, None]
    keys_here = prefill_key_values[0].reshape(pre_rows, kv_heads, HEAD_SIZE)
    values_here = prefill_key_values[1].reshape(pre_rows, kv_heads, HEAD_SIZE)
    query_rows = prefill_query_rows.reshape(pre_rows, kv_heads, head_group, HEAD_SIZE)
    scores = (
        jnp.einsum("qhgd,khd->qhgk", query_rows, keys_here, preferred_element_type=jnp.float32)
        * scale
    )
    places = jnp.arange(pre_rows, dtype=jnp.int32)
    visible = places[None, :] <= places[:, None]
    scores = jnp.where(visible[:, None, None, :], scores, -jnp.inf)
    weight_matrix = softmax_probability(scores, sink_logit_bias)
    pre_out = jnp.einsum(
        "qhgk,khd->qhgd", weight_matrix, values_here, preferred_element_type=jnp.float32
    )
    pre_out = pre_out.astype(jnp.bfloat16).reshape(pre_rows, q_heads * HEAD_SIZE)
    dec_queries = decode_query_rows.reshape(dec_rows, kv_heads, head_group, HEAD_SIZE)
    cached_key_rows = cache[0].reshape(dec_rows, kv_max, kv_heads, HEAD_SIZE)
    cached_value_rows = cache[1].reshape(dec_rows, kv_max, kv_heads, HEAD_SIZE)
    own_key_rows = decode_key_values[0].reshape(dec_rows, kv_heads, HEAD_SIZE)
    own_value_rows = decode_key_values[1].reshape(dec_rows, kv_heads, HEAD_SIZE)
    past_positions = (
        jnp.einsum(
            "shgd,sjhd->shgj", dec_queries, cached_key_rows, preferred_element_type=jnp.float32
        )
        * scale
    )
    live = jnp.arange(kv_max, dtype=jnp.int32)[None, :] < cache_len[:, None]
    past_positions = jnp.where(live[:, None, None, :], past_positions, -jnp.inf)
    own_token = (
        jnp.einsum("shgd,shd->shg", dec_queries, own_key_rows, preferred_element_type=jnp.float32)[
            ..., None
        ]
        * scale
    )
    dec_weights = softmax_probability(
        jnp.concatenate([past_positions, own_token], axis=-1), sink_logit_bias
    )
    dec_out = jnp.einsum(
        "shgj,sjhd->shgd",
        dec_weights[..., :kv_max],
        cached_value_rows,
        preferred_element_type=jnp.float32,
    )
    dec_out = (
        dec_out
        + dec_weights[..., kv_max:].astype(jnp.float32)
        * own_value_rows.astype(jnp.float32)[:, :, None, :]
    )
    dec_out = dec_out.astype(jnp.bfloat16).reshape(dec_rows, q_heads * HEAD_SIZE)
    attn_rows = jnp.concatenate([pre_out, dec_out], axis=0)
    return attn_rows
def general_path(
    x_pre,
    x_dec,
    prefill_query_rows,
    prefill_key_values,
    decode_query_rows,
    decode_key_values,
    cache,
    cache_len,
    sinks,
    o_weight,
    norm_gain,
    expert_ids,
    route_logits,
    w_gate_up,
    w_down,
):
    attn_rows = attention_rows(
        x_pre,
        x_dec,
        prefill_query_rows,
        prefill_key_values,
        decode_query_rows,
        decode_key_values,
        cache,
        cache_len,
        sinks,
    )
    width = x_pre.shape[1]
    resid = jnp.concatenate([x_pre, x_dec], axis=0).astype(jnp.float32)
    half = attn_rows.shape[0] // 2
    mine = lax.axis_index("hp") * half
    head_part = jnp.dot(
        attn_rows,
        lax.all_gather(o_weight, "ep", axis=1, tiled=True),
        preferred_element_type=jnp.float32,
    )
    summed = lax.psum_scatter(head_part, "hp", scatter_dimension=0, tiled=True)
    stream = lax.dynamic_slice_in_dim(resid, mine, half, 0) + summed
    normed = lax.all_gather(rms_norm(stream, norm_gain), "hp", axis=0, tiled=True)
    tokens_here, topk = expert_ids.shape
    holders = lax.axis_size("ep")
    experts = holders // 2
    slot = min(
        tokens_here, 2 * ((3 * max(1, (tokens_here * topk + experts - 1) // experts) + 3) // 4)
    )
    plane = slot // 2
    flat_ids = expert_ids.reshape(-1)
    onehot = (flat_ids[:, None] == jnp.arange(experts, dtype=jnp.int32)[None, :]).astype(jnp.int32)
    rank = jnp.sum(jnp.cumsum(onehot, axis=0) * onehot, axis=1) - 1
    position = (flat_ids * slot + rank).reshape(tokens_here, topk)
    columns = jnp.arange(experts * slot, dtype=jnp.int32)[None, None, :] == position[:, :, None]
    picked_rows = jnp.any(columns, axis=1).T.astype(jnp.bfloat16)
    per_expert = (
        jnp.dot(picked_rows, normed, preferred_element_type=jnp.float32)
        .astype(jnp.bfloat16)
        .reshape(experts, slot, width)
    )
    send = jnp.repeat(per_expert, 2, axis=0)
    own_plane = lax.dynamic_slice_in_dim(send, lax.axis_index("hp") * plane, plane, 1)
    arrived_plane = lax.all_to_all(own_plane, "ep", split_axis=0, concat_axis=0, tiled=True)
    arrived = lax.all_gather(arrived_plane, "hp", axis=1, tiled=True)
    rows = arrived.reshape(-1, width)
    gate = jnp.dot(rows, w_gate_up[0, 0], preferred_element_type=jnp.float32)
    upper = jnp.dot(rows, w_gate_up[0, 1], preferred_element_type=jnp.float32)
    hidden = ((upper + 1.0) * gate * jax.nn.sigmoid(1.702 * gate)).astype(jnp.bfloat16)
    partial_out = jnp.dot(hidden, w_down[0], preferred_element_type=jnp.float32).reshape(
        -1, slot, width
    )
    share = lax.psum_scatter(
        partial_out.astype(jnp.bfloat16), "hp", scatter_dimension=1, tiled=True
    )
    returned = lax.all_to_all(share, "ep", split_axis=0, concat_axis=0, tiled=True)
    mix = jax.nn.softmax(route_logits, axis=-1)
    blend = jnp.sum(jnp.where(columns, mix[:, :, None], 0.0), axis=1).reshape(
        tokens_here, experts, slot
    )
    blend = jnp.repeat(blend, 2, axis=1)
    blend_plane = lax.dynamic_slice_in_dim(blend, lax.axis_index("hp") * plane, plane, 2).reshape(
        tokens_here, holders * plane
    )
    terms = jnp.dot(
        blend_plane,
        returned.reshape(-1, width).astype(jnp.float32),
        precision=lax.Precision.HIGHEST,
    )
    moe = lax.psum_scatter(
        terms.astype(jnp.bfloat16), "hp", scatter_dimension=0, tiled=True
    ).astype(jnp.float32)
    return (stream + moe).astype(jnp.bfloat16)


MESH = pl.DeviceIdType.MESH
SIDE = 2


def layer_kernel(
    depth_z,
    attn_ref,
    wo_ref,
    x_ref,
    gain_ref,
    blend_ref,
    gu_hbm,
    dn_hbm,
    out_ref,
    wo_all,
    mix_all,
    mix_cols,
    attn_all,
    proj,
    proj_in,
    columns,
    kept_rows,
    tok,
    part_out,
    from_core,
    from_first,
    mid,
    from_second,
    to_send,
    from_z,
    gu,
    dn,
    send_sem,
    recv_sem,
    load_sem,
):
    zs = depth_z
    me = lax.axis_index("ep")
    core = lax.axis_index("hp")
    x, y, z = lax.rem(me, 2), lax.rem(me // 2, 2), me // 4
    other = 1 - core
    to_x = {"ep": z * 4 + y * 2 + (1 - x)}
    to_y = {"ep": z * 4 + (1 - y) * 2 + x}
    to_z = [None] + [{"ep": lax.rem(z + d, zs) * 4 + y * 2 + x} for d in range(1, zs)]
    to_core = {"hp": other}

    load_gu = pltpu.make_async_copy(gu_hbm, gu, load_sem.at[0])
    load_dn = pltpu.make_async_copy(dn_hbm, dn, load_sem.at[1])
    load_gu.start()
    load_dn.start()

    barrier = pltpu.get_barrier_semaphore()
    partners = [to_x, to_y, to_core] + to_z[1:]
    for partner in partners:
        pl.semaphore_signal(barrier, inc=1, device_id=partner, device_id_type=MESH)
    for p in range(2):
        wo_all[p, y, x] = wo_ref[p]
    mix_all[z, y, x] = blend_ref[...]
    pl.semaphore_wait(barrier, len(partners))

    sent = []

    def push(source, target, device):
        i = len(sent)
        copy = pltpu.make_async_remote_copy(
            src_ref=source,
            dst_ref=target,
            send_sem=send_sem.at[i],
            recv_sem=recv_sem.at[i],
            device_id=device,
            device_id_type=MESH,
        )
        copy.start()
        sent.append(copy)
        return copy

    def gather(lanes):
        along, second, last = [], [], []
        for view, x_next in lanes:
            own = view(z, y, x)
            along.append([push(own, own, to_z[d]) for d in range(1, zs)])
            second.append([push(own, own, to_x if x_next else to_y)])
            last.append([push(own, own, to_y if x_next else to_x)])
        for d in range(zs):
            zt = lax.rem(z - d + zs, zs)
            for n, (view, x_next) in enumerate(lanes):
                if d:
                    along[n][d - 1].wait_recv()
                    block = view(zt, y, x)
                    second[n].append(push(block, block, to_x if x_next else to_y))
                    last[n].append(push(block, block, to_y if x_next else to_x))
        for d in range(zs):
            zt = lax.rem(z - d + zs, zs)
            for n, (view, x_next) in enumerate(lanes):
                second[n][d].wait_recv()
                block = view(zt, y, 1 - x) if x_next else view(zt, 1 - y, x)
                last[n].append(push(block, block, to_y if x_next else to_x))
        return last

    def settle(across):
        for copies in across:
            for copy in copies:
                copy.wait_recv()

    rows, inner = attn_ref.shape
    half = rows // 2
    split = inner // 2
    width = x_ref.shape[1]
    piece = width // zs
    nt = (((1,), (1,)), ((), ()))

    heads = [push(attn_ref, attn_all.at[d - 1], to_z[d]) for d in range(1, zs)]
    own0, own1 = wo_all.at[0, y, x], wo_all.at[1, y, x]
    weights = [push(own0, own0, to_y), push(own1, own1, to_x)]
    weights += [push(own0, own0, to_x), push(own1, own1, to_y)]
    own = mix_all.at[z, y, x]
    mixes = [push(own, own, to_z[d]) for d in range(1, zs)]
    weights[0].wait_recv()
    near = wo_all.at[0, 1 - y, x]
    weights.append(push(near, near, to_x))
    weights[1].wait_recv()
    near = wo_all.at[1, y, 1 - x]
    weights.append(push(near, near, to_y))
    for copy in mixes:
        copy.wait_recv()
    near = mix_all.at[:, y, x]
    copy = push(near, near, to_y)
    copy.wait_recv()
    near = mix_all.at[:, :, x]
    mixes = push(near, near, to_x)
    for copy in weights[2:]:
        copy.wait_recv()
    exchange = []
    for d in range(zs):
        if d:
            heads[d - 1].wait_recv()
        queries = attn_all[d - 1] if d else attn_ref[...]
        total = 0.0
        for p in range(2):
            total = total + lax.dot_general(
                queries[:, p * split : (p + 1) * split],
                wo_all[p].reshape(piece, split),
                nt,
                preferred_element_type=jnp.float32,
            )
        proj[d, 0] = total[:half]
        proj[d, 1] = total[half:]
        exchange.append(push(proj.at[d, other], proj_in.at[d], to_core))
    returns = []
    for d in list(range(1, zs)) + [0]:
        exchange[d].wait_recv()
        if d:
            proj[d, core] = proj[d, core] + proj_in[d]
            returns.append(push(proj.at[d, core], columns.at[z], to_z[zs - d]))
        else:
            columns[z] = proj[0, core] + proj_in[0]
    mixes.wait_recv()

    expert = me // 2
    experts_rows = jnp.concatenate(
        [
            mix_all[a, b, c, pl.ds(expert, 1), :]
            for a in range(zs)
            for b in range(2)
            for c in range(2)
        ],
        axis=0,
    )
    mix_cols[...] = experts_rows.T

    for copy in returns:
        copy.wait_recv()
    mine = pl.ds(pl.multiple_of(core * half, half), half)
    added = jnp.concatenate([columns[a] for a in range(zs)], axis=1)
    stream = x_ref[mine, :].astype(jnp.float32) + added
    kept_rows[...] = stream
    mean_sq = jnp.mean(stream * stream, axis=-1, keepdims=True)
    normed = (stream * lax.rsqrt(mean_sq + EPS) * gain_ref[...]).astype(jnp.bfloat16)
    r = half // 2
    for p in range(2):
        tok[core, p, z, y, x] = normed[p * r : (p + 1) * r]
    across = gather(
        [
            (lambda *at: tok.at[(core, 0, *at)], True),
            (lambda *at: tok.at[(core, 1, *at)], False),
        ]
    )
    def near(ref, side, p):
        return ref.at[side, 0, :, y] if p == 0 else ref.at[side, 1, :, :, x]

    def far(ref, side, p, zt):
        return ref.at[side, 0, zt, 1 - y] if p == 0 else ref.at[side, 1, zt, :, 1 - x]

    def expert_rows(rows_in, scale):
        gate = jnp.dot(rows_in, gu[0], preferred_element_type=jnp.float32)
        upper = jnp.dot(rows_in, gu[1], preferred_element_type=jnp.float32)
        hidden = (upper + 1.0) * gate * jax.nn.sigmoid(1.702 * gate) * scale
        result = jnp.dot(hidden.astype(jnp.bfloat16), dn[...], preferred_element_type=jnp.float32)
        return result.astype(jnp.bfloat16)

    def scales(side, p, places):
        cols = mix_cols[pl.ds(pl.multiple_of(side * half + p * r, r), r), :]
        lane = lax.broadcasted_iota(jnp.int32, cols.shape, 1)
        return [
            jnp.sum(jnp.where(lane == place, cols, 0.0), axis=1, keepdims=True) for place in places
        ]

    def place(zt, yy, xx):
        return zt * 4 + yy * 2 + xx

    over_near = [push(near(tok, core, p), near(tok, core, p), to_core) for p in range(2)]
    load_gu.wait()
    load_dn.wait()

    def run_near(side):
        rows_in, scale = [], []
        for p in range(2):
            rows_in.append(near(tok, side, p)[...].reshape(2 * zs * r, width))
            scale += scales(
                side,
                p,
                [
                    place(a, y, b) if p == 0 else place(a, b, x)
                    for a in range(zs)
                    for b in range(2)
                ],
            )
        result = expert_rows(jnp.concatenate(rows_in, axis=0), jnp.concatenate(scale, axis=0))
        result = result.reshape(2, zs, 2, r, width)
        for p in range(2):
            near(part_out, side, p)[...] = result[p]

    def arrive(d):
        zt = lax.rem(z - d + zs, zs)
        copies = []
        for p in range(2):
            across[p][d].wait_recv()
            across[p][zs + d].wait_recv()
            copies.append(push(far(tok, core, p, zt), far(tok, core, p, zt), to_core))
        return copies

    def run_far(d, copies):
        zt = lax.rem(z - d + zs, zs)
        for copy in copies:
            copy.wait_recv()
        rows_in, scale = [], []
        for side in (core, other):
            for p in range(2):
                rows_in.append(far(tok, side, p, zt)[...].reshape(2 * r, width))
                scale += scales(
                    side,
                    p,
                    [place(zt, 1 - y, b) if p == 0 else place(zt, b, 1 - x) for b in range(2)],
                )
        result = expert_rows(jnp.concatenate(rows_in, axis=0), jnp.concatenate(scale, axis=0))
        result = result.reshape(2, 2, 2, r, width)
        for n, side in enumerate((core, other)):
            for p in range(2):
                far(part_out, side, p, zt)[...] = result[n, p]
        return [
            push(far(part_out, other, p, zt), from_core.at[p, zs + d], to_core) for p in range(2)
        ]

    def add_far(d, copies):
        zt = lax.rem(z - d + zs, zs)
        started = []
        for p in range(2):
            copies[p].wait_recv()
            block = far(part_out, core, p, zt)
            total = block[...].astype(jnp.float32) + from_core[p, zs + d].astype(jnp.float32)
            block[...] = total.astype(jnp.bfloat16)
            started.append(push(block, from_first.at[p, d], to_y if p == 0 else to_x))
        return started

    run_near(core)
    crossed = [arrive(0)]
    for copy in over_near:
        copy.wait_recv()
    run_near(other)
    near_back = [
        push(near(part_out, other, p), from_core.at[p, pl.ds(0, zs)], to_core) for p in range(2)
    ]
    done, firsts = [], []
    for d in range(zs):
        if d + 1 < zs:
            crossed.append(arrive(d + 1))
        done.append(run_far(d, crossed[d]))
        if d:
            firsts.append(add_far(d - 1, done[d - 1]))
    firsts.append(add_far(zs - 1, done[zs - 1]))
    for p in range(2):
        near_back[p].wait_recv()
    seconds, lasts = [[], []], [[], []]
    for d in range(zs):
        for p in range(2):
            zt = lax.rem(z - d + zs, zs)
            firsts[d][p].wait_recv()
            kept = part_out[core, 0, zt, y] if p == 0 else part_out[core, 1, zt, :, x]
            total = kept.astype(jnp.float32) + from_core[p, zt].astype(jnp.float32)
            total = total + from_first[p, d].astype(jnp.float32)
            mid[p, d] = total.astype(jnp.bfloat16)
            away = mid.at[p, d, 1 - (x if p == 0 else y)]
            seconds[p].append(push(away, from_second.at[p, d], to_x if p == 0 else to_y))
    totals = []
    for d in range(zs):
        for p in range(2):
            seconds[p][d].wait_recv()
            kept = mid[p, d, x if p == 0 else y].astype(jnp.float32)
            total = kept + from_second[p, d].astype(jnp.float32)
            if d:
                to_send[p, d - 1] = total.astype(jnp.bfloat16)
                lasts[p].append(push(to_send.at[p, d - 1], from_z.at[p, d - 1], to_z[zs - d]))
            else:
                totals.append(total)
    for p in range(2):
        total = totals[p]
        for e in range(1, zs):
            lasts[p][e - 1].wait_recv()
            total = total + from_z[p, e - 1].astype(jnp.float32)
        out_ref[p * r : (p + 1) * r, :] = (kept_rows[p * r : (p + 1) * r, :] + total).astype(
            jnp.bfloat16
        )
    for copy in sent:
        copy.wait_send()


def fused_path(
    holders,
    x_pre,
    x_dec,
    prefill_query_rows,
    prefill_key_values,
    decode_query_rows,
    decode_key_values,
    cache,
    cache_len,
    sinks,
    o_weight,
    norm_gain,
    expert_ids,
    route_logits,
    w_gate_up,
    w_down,
):
    attn_rows = attention_rows(
        x_pre,
        x_dec,
        prefill_query_rows,
        prefill_key_values,
        decode_query_rows,
        decode_key_values,
        cache,
        cache_len,
        sinks,
    )
    tokens, inner = attn_rows.shape
    width = x_pre.shape[1]
    hidden = w_down.shape[1]
    columns = o_weight.shape[1]
    zs = holders // 4
    half, r = tokens // 2, tokens // 4
    experts = holders // 2
    resid = jnp.concatenate([x_pre, x_dec], axis=0)
    wo = o_weight.reshape(2, inner // 2, columns).transpose(0, 2, 1)
    mix = jax.nn.softmax(route_logits, axis=-1)
    chosen = expert_ids[None, :, :] == jnp.arange(experts, dtype=jnp.int32)[:, None, None]
    blend = jnp.sum(jnp.where(chosen, mix[None], 0.0), axis=-1)
    blend = jnp.pad(blend, ((0, 0), (0, -tokens % 128)))
    bf = jnp.bfloat16
    grid = (zs, 2, 2)
    return pl.pallas_call(
        functools.partial(layer_kernel, zs),
        out_shape=jax.ShapeDtypeStruct((half, width), bf),
        in_specs=[pl.BlockSpec(memory_space=pltpu.VMEM)] * 5
        + [pl.BlockSpec(memory_space=pl.ANY)] * 2,
        out_specs=pl.BlockSpec(memory_space=pltpu.VMEM),
        scratch_shapes=[
            pltpu.VMEM((2, 2, 2, columns, inner // 2), bf),
            pltpu.VMEM((*grid, *blend.shape), jnp.float32),
            pltpu.VMEM((blend.shape[1], holders), jnp.float32),
            pltpu.VMEM((zs - 1, tokens, inner), bf),
            pltpu.VMEM((zs, 2, half, width // zs), jnp.float32),
            pltpu.VMEM((zs, half, width // zs), jnp.float32),
            pltpu.VMEM((zs, half, width // zs), jnp.float32),
            pltpu.VMEM((half, width), jnp.float32),
            pltpu.VMEM((2, 2, *grid, r, width), bf),
            pltpu.VMEM((2, 2, *grid, r, width), bf),
            pltpu.VMEM((2, 2 * zs, 2, r, width), bf),
            pltpu.VMEM((2, zs, 2, r, width), bf),
            pltpu.VMEM((2, zs, 2, r, width), bf),
            pltpu.VMEM((2, zs, r, width), bf),
            pltpu.VMEM((2, zs - 1, r, width), bf),
            pltpu.VMEM((2, zs - 1, r, width), bf),
            pltpu.VMEM((2, width, hidden), bf),
            pltpu.VMEM((hidden, width), bf),
            pltpu.SemaphoreType.DMA((192,)),
            pltpu.SemaphoreType.DMA((192,)),
            pltpu.SemaphoreType.DMA((2,)),
        ],
        compiler_params=pltpu.CompilerParams(
            collective_id=0, has_side_effects=True, vmem_limit_bytes=60 * 2**20
        ),
    )(attn_rows, wo, resid, norm_gain.reshape(1, width), blend, w_gate_up[0], w_down[0])


def on_device(holders, *args):
    x_pre, x_dec, o_weight = args[0], args[1], args[9]
    tokens = x_pre.shape[0] + x_dec.shape[0]
    gathered = 2 * holders * (tokens * x_pre.shape[1] * 4 + o_weight.size)
    if holders % 4 == 0 and holders >= 8 and tokens % 64 == 0 and gathered < 32 * 2**20:
        return fused_path(holders, *args)
    return general_path(*args)


def solution(mesh):
    placed = (
        P(("groups", "ep"), None),
        P(("groups", "ep"), None),
        P(("groups", "ep"), "hp"),
        P(None, ("groups", "ep"), "hp"),
        P(("groups", "ep"), "hp"),
        P(None, ("groups", "ep"), "hp"),
        P(None, ("groups", "ep"), None, "hp"),
        P(("groups", "ep")),
        P("hp"),
        P("hp", "ep"),
        P(),
        P(("groups", "ep"), None),
        P(("groups", "ep"), None),
        P("ep", None, None, "hp"),
        P("ep", "hp", None),
    )
    return jax.shard_map(
        functools.partial(on_device, mesh.shape["ep"]),
        mesh=mesh,
        in_specs=placed,
        out_specs=P(("groups", "ep", "hp"), None),
        check_vma=False,
    )
```

profile of v0, /device:TPU:0, one launch (start us, length us, event | category | flops | bytes accessed | tf_op | source)
XLA Modules:
  0.0 89.5 jit_solution(14233409240938786467)
XLA Ops:
  0.0 1.1 %fusion.13 = (bf16[1,8,128,128]{3,2,1,0:T(8,128)(2,1)S(1)}, bf16[1,8,128,128]{3,2,1,0:T(8,128)(2,1)S(1)}) fusion(bf16[2,8,128,128]{3,2,1,0:T(8,128)(2,1)} %param.21), kind=kLoop, calls=%fused_computation.37 | loop fusion | bytes 1048576 | tf_op jit(solution)/shard_map/slice | solution.py:62
  1.1 0.2 copy.98
  1.3 0.0 copy-done.6
  1.3 0.1 reshape.100
  1.4 0.2 copy.90
  1.6 0.0 copy-done.10
  1.6 0.1 iota_compare_fusion.2
  1.7 0.3 fusion.15
  2.0 0.0 copy-done.8
  2.0 0.1 reshape.111
  2.0 0.1 fusion.17
  2.2 0.0 copy-done.11
  2.2 0.1 max.32
  2.3 0.2 copy.92
  2.5 0.1 maximum_subtract_fusion
  2.5 0.7 copy.95
  3.2 0.1 exponential_reduce_fusion
  3.4 0.1 divide_convert_fusion
  3.6 0.0 copy-start.2
  3.6 0.0 copy-start.3
  3.6 0.1 reshape.105
  3.7 0.3 fusion.4
  4.0 0.1 reshape.101
  4.1 0.3 copy-done.2
  4.5 0.2 reshape.98
  4.7 0.1 reshape_squeeze.16
  4.8 0.4 fusion.16
  5.2 0.1 broadcast_maximum_fusion
  5.2 0.1 fusion.6
  5.3 0.1 exponential_add_fusion
  5.4 0.1 reshape_squeeze.17
  5.5 0.3 fusion.2
  5.8 0.0 copy-start.1
  5.8 0.0 copy-start.4
  5.8 0.0 copy-start.7
  5.8 0.0 copy-start.5
  5.8 0.0 copy-start.9
  5.9 0.2 reshape.99
  6.1 0.7 pad_maximum_fusion.1.attn_ref
  6.7 0.7 copy.130
  7.4 0.0 copy-done.4
  7.4 0.7 pad_maximum_fusion.x_ref
  8.1 0.6 reshape.103.gain_ref
  8.7 0.0 copy-done.5
  8.8 0.0 copy-done.9
  8.8 0.6 pad.4.blend_ref
  9.4 78.6 %shard_map.145 = bf16[32,1536]{1,0:T(8,128)(2,1)} custom-call(bf16[64,1024]{1,0:T(8,128)(2,1)} %pad_maximum_fusion.1.attn_ref, bf16[2,96,512]{2,1,0:T(8,128)(2,1)} %bitcast.40, bf16[64,1536]{1,0:T(8,128)(2,1)} %pad_maximum_fusion.x_ref, f32[1,1536]{1,0:T(1,128)} %reshape.103.gain_ref, f32[8,128]{1,0:T(8,128)} %pad.4.blend_ref, ...), custom_call_target="tpu_custom_call" | custom-call | tf_op jit(solution)/shard_map/pallas_call | solution.py:559
  88.0 1.5 %copy.132 = bf16[32,1536]{1,0:T(8,128)(2,1)} copy(bf16[32,1536]{1,0:T(8,128)(2,1)} %shard_map.145) | data formatting | bytes 196608
  (23 shorter events, 0.2 us)
Async XLA Ops:
  0.0 1.3 %copy-start.6 = (bf16[8,1024]{1,0:T(8,128)(2,1)S(1)}, bf16[8,1024]{1,0:T(8,128)(2,1)}, u32[]{:S(2)}) copy-start(bf16[8,1024]{1,0:T(8,128)(2,1)} %param.19) | copy-start | bytes 49156
  0.0 1.6 %copy-start.10 = (s32[8]{0:T(128)S(1)}, s32[8]{0:T(128)}, u32[]{:S(2)}) copy-start(s32[8]{0:T(128)} %param.22) | copy-start | bytes 100
  0.0 2.0 %copy-start.8 = (bf16[2,8,128]{2,1,0:T(8,128)(2,1)S(1)}, bf16[2,8,128]{2,1,0:T(8,128)(2,1)}, u32[]{:S(2)}) copy-start(bf16[2,8,128]{2,1,0:T(8,128)(2,1)} %param.20) | copy-start | bytes 12292
  0.0 2.2 %copy-start.11 = (f32[16]{0:T(128)S(1)}, f32[16]{0:T(128)}, u32[]{:S(2)}) copy-start(f32[16]{0:T(128)} %param.23) | copy-start | bytes 196
  3.6 0.9 %copy-start.2 = (bf16[56,1024]{1,0:T(8,128)(2,1)S(1)}, bf16[56,1024]{1,0:T(8,128)(2,1)}, u32[]{:S(2)}) copy-start(bf16[56,1024]{1,0:T(8,128)(2,1)} %param.17) | copy-start | bytes 344068
  3.6 1.1 %copy-start.3 = (bf16[2,56,128]{2,1,0:T(8,128)(2,1)S(1)}, bf16[2,56,128]{2,1,0:T(8,128)(2,1)}, u32[]{:S(2)}) copy-start(bf16[2,56,128]{2,1,0:T(8,128)(2,1)} %param.18) | copy-start | bytes 86020
  5.5 1.2 %copy-start = (bf16[1024,96]{0,1:T(8,128)(2,1)S(1)}, bf16[1024,96]{0,1:T(8,128)(2,1)}, u32[]{:S(2)}) copy-start(bf16[1024,96]{0,1:T(8,128)(2,1)} %param.24) | copy-start | bytes 589828
  5.8 1.6 %copy-start.1 = (bf16[56,1536]{1,0:T(8,128)(2,1)S(1)}, bf16[56,1536]{1,0:T(8,128)(2,1)}, u32[]{:S(2)}) copy-start(bf16[56,1536]{1,0:T(8,128)(2,1)} %param.15) | copy-start | bytes 516100
  5.8 1.6 %copy-start.4 = (bf16[8,1536]{1,0:T(8,128)(2,1)S(1)}, bf16[8,1536]{1,0:T(8,128)(2,1)}, u32[]{:S(2)}) copy-start(bf16[8,1536]{1,0:T(8,128)(2,1)} %param.16) | copy-start | bytes 73732
  5.8 2.3 %copy-start.7 = (f32[1536]{0:T(1024)S(1)}, f32[1536]{0:T(1024)}, u32[]{:S(2)}) copy-start(f32[1536]{0:T(1024)} %param.25) | copy-start | bytes 18436
  5.8 2.9 %copy-start.5 = (f32[64,4]{0,1:T(4,128)S(1)}, f32[64,4]{0,1:T(4,128)}, u32[]{:S(2)}) copy-start(f32[64,4]{0,1:T(4,128)} %param.27) | copy-start | bytes 3076
  5.8 2.9 %copy-start.9 = (s32[64,4]{0,1:T(4,128)S(1)}, s32[64,4]{0,1:T(4,128)}, u32[]{:S(2)}) copy-start(s32[64,4]{0,1:T(4,128)} %param.26) | copy-start | bytes 3076
where the time goes:
time: 89.7 us; the launch traced here: 89.5 us
  Pallas kernels  78.6 us (88%)
  local copies, waits for them, and re-layouts  7.16 us (8%)
  other arithmetic  2.16 us (2%)
  matrix products  1.34 us (1%)
    pallas_call x1, Pallas kernels, fused_path(): pl.pallas_call(functools.partial(layer_kernel, zs), out_shape=jax.ShapeDt...  78.6 us
    unnamed x25, local copies, waits for them, and re-layouts  1.93 us

commit v1 on v0

v1 whole, which is shorter than its diff:
```python
import functools

import jax
import jax.numpy as jnp
from jax import lax
from jax.experimental import pallas as pl
from jax.experimental.pallas import tpu as pltpu
from jax.sharding import PartitionSpec as P

HEAD_SIZE = 64


EPS = 1e-05


def softmax_probability(scores, sink_logit_bias):
    top = jnp.maximum(jnp.max(scores, axis=-1, keepdims=True), sink_logit_bias)
    expo = jnp.exp(scores - top)
    total = jnp.sum(expo, axis=-1, keepdims=True) + jnp.exp(sink_logit_bias - top)
    return (expo / total).astype(jnp.bfloat16)


def rms_norm(stream, gain):
    mean_sq = jnp.mean(stream * stream, axis=-1, keepdims=True)
    return (stream * lax.rsqrt(mean_sq + EPS) * gain).astype(jnp.bfloat16)


def attention_rows(
    x_pre,
    x_dec,
    prefill_query_rows,
    prefill_key_values,
    decode_query_rows,
    decode_key_values,
    cache,
    cache_len,
    sinks):
    pre_rows, width = x_pre.shape
    dec_rows = x_dec.shape[0]
    kv_heads = prefill_key_values.shape[2] // HEAD_SIZE
    q_heads = sinks.shape[0]
    head_group = q_heads // kv_heads
    kv_max = cache.shape[2]
    scale = HEAD_SIZE ** (-0.5)
    sink_logit_bias = sinks.reshape(kv_heads, head_group)[None, :, :, None]
    keys_here = prefill_key_values[0].reshape(pre_rows, kv_heads, HEAD_SIZE)
    values_here = prefill_key_values[1].reshape(pre_rows, kv_heads, HEAD_SIZE)
    query_rows = prefill_query_rows.reshape(pre_rows, kv_heads, head_group, HEAD_SIZE)
    scores = (
        jnp.einsum("qhgd,khd->qhgk", query_rows, keys_here, preferred_element_type=jnp.float32)
        * scale
    )
    places = jnp.arange(pre_rows, dtype=jnp.int32)
    visible = places[None, :] <= places[:, None]
    scores = jnp.where(visible[:, None, None, :], scores, -jnp.inf)
    weight_matrix = softmax_probability(scores, sink_logit_bias)
    pre_out = jnp.einsum(
        "qhgk,khd->qhgd", weight_matrix, values_here, preferred_element_type=jnp.float32
    )
    pre_out = pre_out.astype(jnp.bfloat16).reshape(pre_rows, q_heads * HEAD_SIZE)
    dec_queries = decode_query_rows.reshape(dec_rows, kv_heads, head_group, HEAD_SIZE)
    cached_key_rows = cache[0].reshape(dec_rows, kv_max, kv_heads, HEAD_SIZE)
    cached_value_rows = cache[1].reshape(dec_rows, kv_max, kv_heads, HEAD_SIZE)
    own_key_rows = decode_key_values[0].reshape(dec_rows, kv_heads, HEAD_SIZE)
    own_value_rows = decode_key_values[1].reshape(dec_rows, kv_heads, HEAD_SIZE)
    past_positions = (
        jnp.einsum(
            "shgd,sjhd->shgj", dec_queries, cached_key_rows, preferred_element_type=jnp.float32
        )
        * scale
    )
    live = jnp.arange(kv_max, dtype=jnp.int32)[None, :] < cache_len[:, None]
    past_positions = jnp.where(live[:, None, None, :], past_positions, -jnp.inf)
    own_token = (
        jnp.einsum("shgd,shd->shg", dec_queries, own_key_rows, preferred_element_type=jnp.float32)[
            ..., None
        ]
        * scale
    )
    dec_weights = softmax_probability(
        jnp.concatenate([past_positions, own_token], axis=-1), sink_logit_bias
    )
    dec_out = jnp.einsum(
        "shgj,sjhd->shgd",
        dec_weights[..., :kv_max],
        cached_value_rows,
        preferred_element_type=jnp.float32,
    )
    dec_out = (
        dec_out
        + dec_weights[..., kv_max:].astype(jnp.float32)
        * own_value_rows.astype(jnp.float32)[:, :, None, :]
    )
    dec_out = dec_out.astype(jnp.bfloat16).reshape(dec_rows, q_heads * HEAD_SIZE)
    attn_rows = jnp.concatenate([pre_out, dec_out], axis=0)
    return attn_rows
def general_path(
    x_pre,
    x_dec,
    prefill_query_rows,
    prefill_key_values,
    decode_query_rows,
    decode_key_values,
    cache,
    cache_len,
    sinks,
    o_weight,
    norm_gain,
    expert_ids,
    route_logits,
    w_gate_up,
    w_down,
):
    attn_rows = attention_rows(
        x_pre,
        x_dec,
        prefill_query_rows,
        prefill_key_values,
        decode_query_rows,
        decode_key_values,
        cache,
        cache_len,
        sinks,
    )
    width = x_pre.shape[1]
    resid = jnp.concatenate([x_pre, x_dec], axis=0).astype(jnp.float32)
    half = attn_rows.shape[0] // 2
    mine = lax.axis_index("hp") * half
    head_part = jnp.dot(
        attn_rows,
        lax.all_gather(o_weight, "ep", axis=1, tiled=True),
        preferred_element_type=jnp.float32,
    )
    summed = lax.psum_scatter(head_part, "hp", scatter_dimension=0, tiled=True)
    stream = lax.dynamic_slice_in_dim(resid, mine, half, 0) + summed
    normed = lax.all_gather(rms_norm(stream, norm_gain), "hp", axis=0, tiled=True)
    tokens_here, topk = expert_ids.shape
    holders = lax.axis_size("ep")
    experts = holders // 2
    slot = min(
        tokens_here, 2 * ((3 * max(1, (tokens_here * topk + experts - 1) // experts) + 3) // 4)
    )
    plane = slot // 2
    flat_ids = expert_ids.reshape(-1)
    onehot = (flat_ids[:, None] == jnp.arange(experts, dtype=jnp.int32)[None, :]).astype(jnp.int32)
    rank = jnp.sum(jnp.cumsum(onehot, axis=0) * onehot, axis=1) - 1
    position = (flat_ids * slot + rank).reshape(tokens_here, topk)
    columns = jnp.arange(experts * slot, dtype=jnp.int32)[None, None, :] == position[:, :, None]
    picked_rows = jnp.any(columns, axis=1).T.astype(jnp.bfloat16)
    per_expert = (
        jnp.dot(picked_rows, normed, preferred_element_type=jnp.float32)
        .astype(jnp.bfloat16)
        .reshape(experts, slot, width)
    )
    send = jnp.repeat(per_expert, 2, axis=0)
    own_plane = lax.dynamic_slice_in_dim(send, lax.axis_index("hp") * plane, plane, 1)
    arrived_plane = lax.all_to_all(own_plane, "ep", split_axis=0, concat_axis=0, tiled=True)
    arrived = lax.all_gather(arrived_plane, "hp", axis=1, tiled=True)
    rows = arrived.reshape(-1, width)
    gate = jnp.dot(rows, w_gate_up[0, 0], preferred_element_type=jnp.float32)
    upper = jnp.dot(rows, w_gate_up[0, 1], preferred_element_type=jnp.float32)
    hidden = ((upper + 1.0) * gate * jax.nn.sigmoid(1.702 * gate)).astype(jnp.bfloat16)
    partial_out = jnp.dot(hidden, w_down[0], preferred_element_type=jnp.float32).reshape(
        -1, slot, width
    )
    share = lax.psum_scatter(
        partial_out.astype(jnp.bfloat16), "hp", scatter_dimension=1, tiled=True
    )
    returned = lax.all_to_all(share, "ep", split_axis=0, concat_axis=0, tiled=True)
    mix = jax.nn.softmax(route_logits, axis=-1)
    blend = jnp.sum(jnp.where(columns, mix[:, :, None], 0.0), axis=1).reshape(
        tokens_here, experts, slot
    )
    blend = jnp.repeat(blend, 2, axis=1)
    blend_plane = lax.dynamic_slice_in_dim(blend, lax.axis_index("hp") * plane, plane, 2).reshape(
        tokens_here, holders * plane
    )
    terms = jnp.dot(
        blend_plane,
        returned.reshape(-1, width).astype(jnp.float32),
        precision=lax.Precision.HIGHEST,
    )
    moe = lax.psum_scatter(
        terms.astype(jnp.bfloat16), "hp", scatter_dimension=0, tiled=True
    ).astype(jnp.float32)
    return (stream + moe).astype(jnp.bfloat16)


MESH = pl.DeviceIdType.MESH
LANES = 128
NT = (((1,), (1,)), ((), ()))


def f32_dot(a, b):
    return jnp.dot(a, b, preferred_element_type=jnp.float32)


def f32_dot_nt(a, b):
    return lax.dot_general(a, b, NT, preferred_element_type=jnp.float32)


def layer_kernel(
    xp_hbm,
    xd_hbm,
    qp_hbm,
    kvp_hbm,
    qd_hbm,
    kvd_hbm,
    cache_hbm,
    lens_hbm,
    sinks_hbm,
    wo_hbm,
    gain_hbm,
    ids_hbm,
    logits_hbm,
    gu_hbm,
    dn_hbm,
    out_ref,
    xp,
    xd,
    qp,
    kvp,
    qd,
    kvd,
    cache,
    lens,
    sinks,
    gain,
    ids,
    logits,
    gu,
    dn,
    wo_all,
    mix_all,
    mix_cols,
    attn_all,
    proj,
    proj_in,
    ret,
    columns,
    kept_rows,
    tok,
    part_out,
    from_core,
    from_first,
    mid,
    from_second,
    to_send,
    from_z,
    send_sem,
    recv_sem,
    load_sem,
):
    me = lax.axis_index("ep")
    core = lax.axis_index("hp")
    x, y, z = lax.rem(me, 2), lax.rem(me // 2, 2), me // 4
    zl, zh = lax.rem(z, 2), z // 2
    other = 1 - core
    zk = [z, zh * 2 + 1 - zl, (1 - zh) * 2 + zl, (1 - zh) * 2 + 1 - zl]
    to_x = {"ep": z * 4 + y * 2 + (1 - x)}
    to_y = {"ep": z * 4 + (1 - y) * 2 + x}
    to_z = [None] + [{"ep": zk[k] * 4 + y * 2 + x} for k in range(1, 4)]
    to_core = {"hp": other}

    loads = []

    def load(source, target):
        copy = pltpu.make_async_copy(source, target, load_sem.at[len(loads)])
        copy.start()
        loads.append(copy)
        return copy

    load_wo = load(wo_hbm, wo_all.at[y, x])
    load_lens = load(lens_hbm, lens)
    load_sinks = load(sinks_hbm, sinks)
    load_qp = load(qp_hbm, qp)
    load_kvp = load(kvp_hbm, kvp)
    load_qd = load(qd_hbm, qd)
    load_kvd = load(kvd_hbm, kvd)
    load_cache = load(cache_hbm, cache)
    load_ids = load(ids_hbm, ids)
    load_logits = load(logits_hbm, logits)
    load_xp = load(xp_hbm, xp)
    load_xd = load(xd_hbm, xd)
    load_gain = load(gain_hbm, gain)
    load_gu = load(gu_hbm, gu)
    load_dn = load(dn_hbm, dn)

    barrier = pltpu.get_barrier_semaphore()
    partners = [to_x, to_y, to_core] + to_z[1:]
    for partner in partners:
        pl.semaphore_signal(barrier, inc=1, device_id=partner, device_id_type=MESH)
    pl.semaphore_wait(barrier, len(partners))

    sent = []

    def push(source, target, device):
        i = len(sent)
        copy = pltpu.make_async_remote_copy(
            src_ref=source,
            dst_ref=target,
            send_sem=send_sem.at[i],
            recv_sem=recv_sem.at[i],
            device_id=device,
            device_id_type=MESH,
        )
        copy.start()
        sent.append(copy)
        return copy

    def send(block, device):
        return push(block, block, device)

    bf = jnp.bfloat16
    f32 = jnp.float32

    load_wo.wait()
    cols = wo_all.shape[2]
    piece = cols // 2
    wo_part = lambda yy, xx, p: wo_all.at[yy, xx, pl.ds(p * piece, piece)]
    wo_first = [send(wo_part(y, x, 0), to_y), send(wo_part(y, x, 1), to_x)]
    wo_last = [send(wo_part(y, x, 0), to_x), send(wo_part(y, x, 1), to_y)]

    tokens = logits.shape[1]
    experts = mix_all.shape[4]
    load_ids.wait()
    load_logits.wait()
    scores = logits[...]
    raised = jnp.exp(scores - jnp.max(scores, axis=0, keepdims=True))
    mix = raised / jnp.sum(raised, axis=0, keepdims=True)
    named = ids[...]
    expert_row = lax.broadcasted_iota(jnp.int32, (experts, tokens), 0)
    blend = jnp.zeros((experts, tokens), f32)
    for k in range(named.shape[0]):
        blend = blend + jnp.where(expert_row == named[k : k + 1], mix[k : k + 1], 0.0)
    spare = mix_all.shape[5] - tokens
    if spare:
        blend = jnp.concatenate([blend, jnp.zeros((experts, spare), f32)], axis=1)
    mix_all[zh, zl, y, x] = blend
    mix_copy = send(mix_all.at[zh, zl, y, x], to_x)

    scale = HEAD_SIZE ** (-0.5)
    kv_heads = kvp.shape[2] // HEAD_SIZE
    pre = qp.shape[0]
    dec = qd.shape[0]
    inner = qp.shape[1]
    pairs = inner // LANES
    per_kv = pairs // kv_heads
    low1 = lax.broadcasted_iota(jnp.int32, (1, LANES), 1) < HEAD_SIZE
    for copy in (load_lens, load_sinks, load_qp, load_kvp, load_qd, load_kvd):
        copy.wait()

    def half_lanes(shape):
        return lax.broadcasted_iota(jnp.int32, shape, len(shape) - 1) < HEAD_SIZE

    def doubled(rows, j):
        turned = pltpu.roll(rows, HEAD_SIZE, 1)
        low = half_lanes(rows.shape)
        even, odd = (rows, turned) if j == 0 else (turned, rows)
        gap = jnp.zeros((HEAD_SIZE - pre, LANES), f32)
        stack = [jnp.where(low, even, 0.0)]
        if HEAD_SIZE > pre:
            stack.append(gap)
        stack.append(jnp.where(low, 0.0, odd))
        if HEAD_SIZE > pre:
            stack.append(gap)
        return jnp.concatenate(stack, axis=0).astype(bf)

    def prefill(j):
        keys = doubled(kvp[0].astype(f32), j)
        values = doubled(kvp[1].astype(f32), j)
        queries = jnp.concatenate(
            [
                qp[:, i * LANES : (i + 1) * LANES].astype(f32)
                for i in range(j * per_kv, (j + 1) * per_kv)
            ],
            axis=0,
        ).astype(bf)
        products = f32_dot_nt(queries, keys) * scale
        shape = (pre, LANES)
        low = half_lanes(shape)
        key_at = lax.broadcasted_iota(jnp.int32, shape, 1)
        key_at = jnp.where(low, key_at, key_at - HEAD_SIZE)
        seen = key_at <= lax.broadcasted_iota(jnp.int32, shape, 0)
        weights = []
        for n in range(per_kv):
            head = 2 * (j * per_kv + n)
            sink_even, sink_odd = sinks[head], sinks[head + 1]
            s = jnp.where(seen, products[n * pre : (n + 1) * pre], -jnp.inf)
            top_even = jnp.max(jnp.where(low, s, -jnp.inf), axis=1, keepdims=True)
            top_odd = jnp.max(jnp.where(low, -jnp.inf, s), axis=1, keepdims=True)
            top_even = jnp.maximum(top_even, sink_even)
            top_odd = jnp.maximum(top_odd, sink_odd)
            expo = jnp.exp(s - jnp.where(low, top_even, top_odd))
            sum_even = jnp.sum(jnp.where(low, expo, 0.0), axis=1, keepdims=True)
            sum_odd = jnp.sum(jnp.where(low, 0.0, expo), axis=1, keepdims=True)
            sum_even = sum_even + jnp.exp(sink_even - top_even)
            sum_odd = sum_odd + jnp.exp(sink_odd - top_odd)
            weights.append(expo / jnp.where(low, sum_even, sum_odd))
        weights = jnp.concatenate(weights, axis=0).astype(bf)
        return f32_dot(weights, values)

    def decode():
        kv_max = cache.shape[2]
        lane = half_lanes((dec, LANES))
        even, odd = [], []
        for i in range(pairs):
            block = qd[:, i * LANES : (i + 1) * LANES].astype(f32)
            turned = pltpu.roll(block, HEAD_SIZE, 1)
            if i < per_kv:
                even.append(jnp.where(lane, block, 0.0))
                odd.append(jnp.where(lane, turned, 0.0))
            else:
                even.append(jnp.where(lane, 0.0, turned))
                odd.append(jnp.where(lane, 0.0, block))
        queries = jnp.concatenate(even + odd, axis=0)
        rows = queries.shape[0]
        groups = rows // dec
        row_seq = lax.rem(lax.broadcasted_iota(jnp.int32, (rows, LANES), 0), dec)
        load_cache.wait()
        products = jnp.zeros((rows, kv_max), f32)
        for s in range(dec):
            mine = jnp.where(row_seq == s, queries, 0.0).astype(bf)
            products = products + f32_dot_nt(mine, cache[0, s])
        grouped = (groups, dec, kv_max)
        products = products.reshape(grouped) * scale
        seq = lax.broadcasted_iota(jnp.int32, (dec, kv_max), 0)
        limit = jnp.zeros((dec, kv_max), jnp.int32)
        for s in range(dec):
            limit = jnp.where(seq == s, lens[s], limit)
        live = lax.broadcasted_iota(jnp.int32, (dec, kv_max), 1) < limit
        products = jnp.where(live[None], products, -jnp.inf)
        own_key = kvd[0].astype(f32)
        own_value = kvd[1].astype(f32)
        own = jnp.sum(queries.reshape(groups, dec, LANES) * own_key[None], axis=2, keepdims=True)
        own = own * scale
        sink = jnp.concatenate(
            [jnp.full((1, dec, 1), sinks[2 * i + odd_head], f32) for odd_head in range(2) for i in range(pairs)],
            axis=0,
        )
        top = jnp.maximum(jnp.max(products, axis=2, keepdims=True), own)
        top = jnp.maximum(top, sink)
        expo = jnp.exp(products - top)
        own_expo = jnp.exp(own - top)
        total = jnp.sum(expo, axis=2, keepdims=True) + own_expo + jnp.exp(sink - top)
        weights = (expo / total).reshape(rows, kv_max)
        own_weight = (own_expo / total).astype(bf).astype(f32)
        summed = jnp.zeros((rows, LANES), f32)
        row_seq = lax.rem(lax.broadcasted_iota(jnp.int32, (rows, kv_max), 0), dec)
        for s in range(dec):
            mine = jnp.where(row_seq == s, weights, 0.0).astype(bf)
            summed = summed + f32_dot(mine, cache[1, s])
        summed = summed.reshape(groups, dec, LANES) + own_weight * own_value[None]
        out = []
        for i in range(pairs):
            a, b = summed[i], summed[pairs + i]
            if i < per_kv:
                out.append(jnp.where(lane, a, pltpu.roll(b, HEAD_SIZE, 1)))
            else:
                out.append(jnp.where(lane, pltpu.roll(a, HEAD_SIZE, 1), b))
        return out

    def keep_attention(j, pre_out, dec_out):
        for n in range(per_kv):
            block = jnp.concatenate(
                [pre_out[n * pre : (n + 1) * pre], dec_out[j * per_kv + n]], axis=0
            )
            attn_all[0, j, :, n * LANES : (n + 1) * LANES] = block.astype(bf)

    heads = [None, [], [], []]

    def send_attention(j):
        heads[2].append(push(attn_all.at[0, j], attn_all.at[2, j], to_z[2]))
        heads[1].append(push(attn_all.at[0, j], attn_all.at[1, j], to_z[1]))

    pre_out = prefill(0)
    dec_out = decode()
    keep_attention(0, pre_out, dec_out)
    send_attention(0)
    for j in range(1, kv_heads):
        keep_attention(j, prefill(j), dec_out)
        send_attention(j)

    mix_copy.wait_recv()
    mix_copy = send(mix_all.at[zh, zl, y], to_y)
    wo_first[0].wait_recv()
    wo_last.append(send(wo_part(1 - y, x, 0), to_x))
    wo_first[1].wait_recv()
    wo_last.append(send(wo_part(y, 1 - x, 1), to_y))
    mix_copy.wait_recv()
    mix_copy = send(mix_all.at[zh, zl], to_z[1])
    heads[2][0].wait_recv()
    heads[3].append(push(attn_all.at[2, 0], attn_all.at[3, 0], to_z[1]))
    for copy in wo_last:
        copy.wait_recv()

    half = tokens // 2
    width = xp.shape[1]
    part = inner // kv_heads

    exchange = []

    def project(k):
        total = 0.0
        for j in range(kv_heads):
            weight = wo_all[:, :, :, j * part : (j + 1) * part].reshape(4 * cols, part)
            total = total + f32_dot_nt(attn_all[k, j], weight)
        proj[k, 0] = total[:half]
        proj[k, 1] = total[half:]
        exchange.append(push(proj.at[k, other], proj_in.at[k], to_core))

    returns = []

    def give_back(k):
        exchange[k].wait_recv()
        total = (proj[k, core] + proj_in[k]).astype(bf)
        if k:
            ret[k - 1] = total
            returns.append(push(ret.at[k - 1], columns.at[z], to_z[k]))
        else:
            columns[z] = total

    project(0)
    for copy in heads[1]:
        copy.wait_recv()
    project(1)
    for j in range(1, kv_heads):
        heads[2][j].wait_recv()
        heads[3].append(push(attn_all.at[2, j], attn_all.at[3, j], to_z[1]))
    project(2)
    give_back(1)
    give_back(2)
    give_back(0)
    mix_copy.wait_recv()
    mix_copy = send(mix_all.at[zh], to_z[2])
    for copy in heads[3]:
        copy.wait_recv()
    project(3)
    give_back(3)

    for copy in (load_xp, load_xd, load_gain):
        copy.wait()
    rest = pre - half
    first_rows = xp[:half].astype(f32)
    last_rows = jnp.concatenate([xp[half:].astype(f32), xd[...].astype(f32)], axis=0)
    resid = jnp.where(core == 0, first_rows, last_rows)
    mix_copy.wait_recv()
    expert = me // 2
    mix_cols[...] = jnp.concatenate(
        [
            mix_all[a, b, c, d, pl.ds(expert, 1), :]
            for a in range(2)
            for b in range(2)
            for c in range(2)
            for d in range(2)
        ],
        axis=0,
    ).T
    for copy in returns:
        copy.wait_recv()
    added = jnp.concatenate([columns[a].astype(f32) for a in range(4)], axis=1)
    stream = resid + added
    kept_rows[...] = stream
    mean_sq = jnp.mean(stream * stream, axis=-1, keepdims=True)
    normed = (stream * lax.rsqrt(mean_sq + EPS) * gain[...][None, :]).astype(bf)
    r = half // 2
    for p in range(2):
        tok[core, p, z, y, x] = normed[p * r : (p + 1) * r]

    def near(ref, p):
        return ref.at[0, y] if p == 0 else ref.at[1, :, x]

    def far(ref, p):
        return ref.at[0, 1 - y] if p == 0 else ref.at[1, :, 1 - x]

    def plane(k, side):
        return tok.at[side, :, zk[k]]

    own = tok.at[core, :, z, y, x]
    along = [None, None, send(own, to_z[2]), None]
    along[1] = send(own, to_z[1])
    steps = [to_x, to_y]
    second, last = [], []
    over = [[] for _ in range(4)]

    def spread(k):
        blocks = [tok.at[core, p, zk[k], y, x] for p in range(2)]
        second.append([send(blocks[0], to_x), send(blocks[1], to_y)])
        last.append([send(blocks[0], to_y), send(blocks[1], to_x)])

    def relay(k):
        second[k][0].wait_recv()
        last[k].append(send(tok.at[core, 0, zk[k], y, 1 - x], to_y))
        second[k][1].wait_recv()
        last[k].append(send(tok.at[core, 1, zk[k], 1 - y, x], to_x))
        for p in range(2):
            over[k].append(send(near(plane(k, core), p), to_core))

    def finish(k):
        for copy in last[k]:
            copy.wait_recv()
        for p in range(2):
            over[k].append(send(far(plane(k, core), p), to_core))

    back = [None] * 4

    def compute(k):
        for copy in over[k]:
            copy.wait_recv()
        rows_in = tok[:, :, zk[k]].reshape(16 * r, width)
        lane = lax.broadcasted_iota(jnp.int32, (r, mix_cols.shape[1]), 1)
        factors = []
        for side in range(2):
            for p in range(2):
                at = side * half + p * r
                table = mix_cols[at : at + r, :]
                for spot in range(4):
                    chosen = jnp.where(lane == zk[k] * 4 + spot, table, 0.0)
                    factors.append(jnp.sum(chosen, axis=1, keepdims=True))
        factor = jnp.concatenate(factors, axis=0)
        gate = f32_dot(rows_in, gu[0])
        upper = f32_dot(rows_in, gu[1])
        hidden = (upper + 1.0) * gate * jax.nn.sigmoid(1.702 * gate) * factor
        result = f32_dot(hidden.astype(bf), dn[...]).astype(bf)
        part_out[k] = result.reshape(2, 2, 2, 2, r, width)
        theirs, target = part_out.at[k, other], from_core.at[k]
        back[k] = [push(far(theirs, p), far(target, p), to_core) for p in range(2)]
        back[k] += [push(near(theirs, p), near(target, p), to_core) for p in range(2)]

    firsts, seconds, lasts = [None] * 4, [None] * 4, [None] * 4

    def first(k):
        firsts[k] = []
        for p in range(2):
            back[k][p].wait_recv()
            block = far(part_out.at[k, core], p)
            total = block[...].astype(f32) + far(from_core.at[k], p)[...].astype(f32)
            block[...] = total.astype(bf)
            firsts[k].append(push(block, from_first.at[k, p], to_y if p == 0 else to_x))

    def reduce_second(k):
        seconds[k] = []
        for p in range(2):
            back[k][2 + p].wait_recv()
            firsts[k][p].wait_recv()
            total = near(part_out.at[k, core], p)[...].astype(f32)
            total = total + near(from_core.at[k], p)[...].astype(f32)
            total = total + from_first[k, p].astype(f32)
            mid[k, p] = total.astype(bf)
            away = mid.at[k, p, 1 - (x if p == 0 else y)]
            seconds[k].append(push(away, from_second.at[k, p], to_x if p == 0 else to_y))

    def reduce_third(k):
        totals = []
        for p in range(2):
            seconds[k][p].wait_recv()
            kept = mid[k, p, x if p == 0 else y].astype(f32)
            totals.append(kept + from_second[k, p].astype(f32))
        if k:
            for p in range(2):
                to_send[k - 1, p] = totals[p].astype(bf)
            lasts[k] = push(to_send.at[k - 1], from_z.at[k - 1], to_z[k])
        return totals

    spread(0)
    relay(0)
    along[1].wait_recv()
    spread(1)
    finish(0)
    along[2].wait_recv()
    along[3] = send(tok.at[core, :, zk[2], y, x], to_z[1])
    spread(2)
    relay(1)
    load_gu.wait()
    load_dn.wait()
    compute(0)
    finish(1)
    along[3].wait_recv()
    spread(3)
    relay(2)
    compute(1)
    finish(2)
    relay(3)
    first(1)
    compute(2)
    finish(3)
    first(2)
    reduce_second(1)
    compute(3)
    reduce_third(1)
    reduce_second(2)
    first(3)
    first(0)
    reduce_third(2)
    reduce_second(3)
    reduce_second(0)
    reduce_third(3)
    totals = reduce_third(0)
    for k in range(1, 4):
        lasts[k].wait_recv()
    for p in range(2):
        total = kept_rows[p * r : (p + 1) * r, :] + totals[p]
        for k in range(1, 4):
            total = total + from_z[k - 1, p].astype(f32)
        out_ref[p * r : (p + 1) * r, :] = total.astype(bf)
    for copy in sent:
        copy.wait_send()


def fused_path(
    holders,
    x_pre,
    x_dec,
    prefill_query_rows,
    prefill_key_values,
    decode_query_rows,
    decode_key_values,
    cache,
    cache_len,
    sinks,
    o_weight,
    norm_gain,
    expert_ids,
    route_logits,
    w_gate_up,
    w_down,
):
    tokens, topk = expert_ids.shape
    width = x_pre.shape[1]
    inner, columns = o_weight.shape
    hidden = w_down.shape[1]
    half, r = tokens // 2, tokens // 4
    experts = holders // 2
    kv_heads = prefill_key_values.shape[2] // HEAD_SIZE
    lanes = -(-tokens // LANES) * LANES
    bf, f32 = jnp.bfloat16, jnp.float32
    operands = (
        x_pre,
        x_dec,
        prefill_query_rows,
        prefill_key_values,
        decode_query_rows,
        decode_key_values,
        cache,
        cache_len,
        sinks,
        o_weight.T,
        norm_gain,
        expert_ids.T,
        route_logits.T,
        w_gate_up[0],
        w_down[0],
    )
    grid = (4, 2, 2)
    return pl.pallas_call(
        layer_kernel,
        out_shape=jax.ShapeDtypeStruct((half, width), bf),
        in_specs=[pl.BlockSpec(memory_space=pl.ANY)] * len(operands),
        out_specs=pl.BlockSpec(memory_space=pltpu.VMEM),
        scratch_shapes=[
            pltpu.VMEM(x_pre.shape, bf),
            pltpu.VMEM(x_dec.shape, bf),
            pltpu.VMEM(prefill_query_rows.shape, bf),
            pltpu.VMEM(prefill_key_values.shape, bf),
            pltpu.VMEM(decode_query_rows.shape, bf),
            pltpu.VMEM(decode_key_values.shape, bf),
            pltpu.VMEM(cache.shape, bf),
            pltpu.SMEM(cache_len.shape, jnp.int32),
            pltpu.SMEM(sinks.shape, f32),
            pltpu.VMEM(norm_gain.shape, f32),
            pltpu.VMEM((topk, tokens), jnp.int32),
            pltpu.VMEM((topk, tokens), f32),
            pltpu.VMEM((2, width, hidden), bf),
            pltpu.VMEM((hidden, width), bf),
            pltpu.VMEM((2, 2, columns, inner), bf),
            pltpu.VMEM((2, 2, 2, 2, experts, lanes), f32),
            pltpu.VMEM((lanes, holders), f32),
            pltpu.VMEM((4, kv_heads, tokens, inner // kv_heads), bf),
            pltpu.VMEM((4, 2, half, width // 4), f32),
            pltpu.VMEM((4, half, width // 4), f32),
            pltpu.VMEM((3, half, width // 4), bf),
            pltpu.VMEM((4, half, width // 4), bf),
            pltpu.VMEM((half, width), f32),
            pltpu.VMEM((2, 2, *grid, r, width), bf),
            pltpu.VMEM((4, 2, 2, 2, 2, r, width), bf),
            pltpu.VMEM((4, 2, 2, 2, r, width), bf),
            pltpu.VMEM((4, 2, 2, r, width), bf),
            pltpu.VMEM((4, 2, 2, r, width), bf),
            pltpu.VMEM((4, 2, r, width), bf),
            pltpu.VMEM((3, 2, r, width), bf),
            pltpu.VMEM((3, 2, r, width), bf),
            pltpu.SemaphoreType.DMA((128,)),
            pltpu.SemaphoreType.DMA((128,)),
            pltpu.SemaphoreType.DMA((16,)),
        ],
        compiler_params=pltpu.CompilerParams(
            collective_id=0, has_side_effects=True, vmem_limit_bytes=60 * 2**20
        ),
    )(*operands)


def on_device(holders, *args):
    x_pre, x_dec, query_rows, key_values, o_weight = args[0], args[1], args[2], args[3], args[9]
    pre, dec = x_pre.shape[0], x_dec.shape[0]
    tokens, width = pre + dec, x_pre.shape[1]
    gathered = 2 * holders * (tokens * width * 4 + o_weight.size)
    fits = (
        holders == 16
        and tokens == HEAD_SIZE
        and pre % 8 == 0
        and dec == 8
        and tokens // 2 <= pre
        and key_values.shape[2] == LANES
        and query_rows.shape[1] % (4 * LANES) == 0
        and args[6].shape[2] == LANES
        and width % (4 * LANES) == 0
        and o_weight.shape[1] % 32 == 0
        and gathered < 32 * 2**20
    )
    if fits:
        return fused_path(holders, *args)
    return general_path(*args)


def solution(mesh):
    placed = (
        P(("groups", "ep"), None),
        P(("groups", "ep"), None),
        P(("groups", "ep"), "hp"),
        P(None, ("groups", "ep"), "hp"),
        P(("groups", "ep"), "hp"),
        P(None, ("groups", "ep"), "hp"),
        P(None, ("groups", "ep"), None, "hp"),
        P(("groups", "ep")),
        P("hp"),
        P("hp", "ep"),
        P(),
        P(("groups", "ep"), None),
        P(("groups", "ep"), None),
        P("ep", None, None, "hp"),
        P("ep", "hp", None),
    )
    return jax.shard_map(
        functools.partial(on_device, mesh.shape["ep"]),
        mesh=mesh,
        in_specs=placed,
        out_specs=P(("groups", "ep", "hp"), None),
        check_vma=False,
    )
```

time: 89.7 us -> 66.7 us (0.74)
  Pallas kernels: 78.6 us -> 65 us
  local copies, waits for them, and re-layouts: 7.16 us -> 1.54 us
  other arithmetic: 2.16 us -> 0 us
  matrix products: 1.34 us -> 0 us
    pallas_call x1, Pallas kernels: 78.6 us -> 65 us  [fused_path(): pl.pallas_call(layer_kernel, out_shape=jax.ShapeDtypeStruct((half, width)...]
    reshape x6 -> x0, local copies, waits for them, and re-layouts: 1.84 us -> none  [the longest x1 0.68 us: fused_path(): wo = o_weight.reshape(2, inner // 2, columns).transpose(0, 2, 1)]
    slice x5 -> x0, local copies, waits for them, and re-layouts: 1.51 us -> none  [the longest x2 1.3 us: attention_rows(): cached_key_rows = cache[0].reshape(dec_rows, kv_max, kv_heads, HEAD_SIZE)]
    concatenate x2 -> x0, other arithmetic: 1.35 us -> none  [the longest x1 0.69 us: fused_path(): resid = jnp.concatenate([x_pre, x_dec], axis=0)]
    dot_general x5 -> x0, matrix products: 1.34 us -> none  [the longest x1 0.37 us: attention_rows(): jnp.einsum('qhgd,khd->qhgk', query_rows, keys_here, preferred_element_typ...]
    unnamed x25 -> x1, local copies, waits for them, and re-layouts: 1.93 us -> 1.54 us
where the time goes in v1:
time: 66.7 us; the launch traced here: 66.5 us
  Pallas kernels  65 us (97%)
  local copies, waits for them, and re-layouts  1.54 us (2%)
    pallas_call x1, Pallas kernels, fused_path(): pl.pallas_call(layer_kernel, out_shape=jax.ShapeDtypeStruct((half, width)...  65 us
    unnamed x1, local copies, waits for them, and re-layouts  1.54 us

profile of v1, /device:TPU:0, one launch (start us, length us, event | category | flops | bytes accessed | tf_op | source)
XLA Modules:
  0.0 66.5 jit_solution(14340990400891499260)
XLA Ops:
  0.0 65.0 %shard_map.145 = bf16[32,1536]{1,0:T(8,128)(2,1)} custom-call(bf16[56,1536]{1,0:T(8,128)(2,1)} %xp_hbm.1, bf16[8,1536]{1,0:T(8,128)(2,1)} %xd_hbm.1, bf16[56,1024]{1,0:T(8,128)(2,1)} %qp_hbm.1, bf16[2,56,128]{2,1,0:T(8,128)(2,1)} %kvp_hbm.1, bf16[8,1024]{1,0:T(8,128)(2,1)} %qd_hbm.1, bf16[2,8,128]{2,1,0:T(8,128)(2,1)} %kvd_hbm.1, ...), custom_call_target="tpu_custom_call" | custom-call | tf_op jit(solution)/shard_map/pallas_call | solution.py:755
  65.0 1.5 %copy.17 = bf16[32,1536]{1,0:T(8,128)(2,1)} copy(bf16[32,1536]{1,0:T(8,128)(2,1)} %shard_map.145) | data formatting | bytes 196608
